TPU v7x, 32 devices: a whole 2x2x4 slice. The times are simulated.
32 devices in a mesh: segment: 4 (over y, core), dp: 8 (over z, x).
Axes of the slice: x: 2, y: 2, z: 4, core: 2. Of those that a mesh axis runs over, the one named last changes fastest.
Arguments:
- token_ids: int32 [1024], P('dp'), may hold values from 0 to 38015, as said below
- table: bfloat16 [4752, 28672], P('segment', 'dp'), may hold values from -6 to 6
- out_grad: bfloat16 [1024, 3584], P('dp', 'segment'), may hold values from -6 to 6
Outputs:
- embedded: bfloat16 [1024, 3584], P('dp')
- table_grad: bfloat16 [4752, 28672], P('segment', 'dp')
Inputs may be any that keep to these rules, and one draw needn't show every extreme that they name: `token_ids`: in the 128 tokens of each data group, at most 16 ids lie in one segment's slice of 9504 rows with one residue modulo 8; in every data group some segment and residue has exactly 16.
All inputs are finite; a program needn't handle non-finite values.
Results may differ from a plain program's by a relative error of at most 0.001.
Values may be sent and summed in bfloat16 or wider, within the bound.
A program may use at most 64 MiB of HBM per device.

v0:
```python
import jax
import jax.numpy as jnp
from jax import lax
from jax.sharding import PartitionSpec as P

D = 3584
PACK = 8


def body(token_ids, table, out_grad):
    lines = table.shape[0]
    width = table.shape[1]
    groups = lax.axis_size("dp")
    tok_rows = token_ids.shape[0]
    quarters = D // width
    slot = lax.axis_index("dp") // quarters
    first = lax.axis_index("segment") * lines * PACK
    every_id = lax.all_gather(token_ids, "dp", axis=0, tiled=True)
    local = every_id - first
    in_section = (local >= 0) & (local < lines * PACK)
    owned = in_section & (local % PACK == slot)
    line_idx = jnp.clip(local // PACK, 0, lines - 1)
    whole_grad = lax.all_gather(out_grad, "segment", axis=1, tiled=True)
    capacity = tok_rows // PACK
    owned_grid = owned.reshape(groups, tok_rows)
    rank = jnp.cumsum(owned_grid.astype(jnp.int32), axis=1) - 1
    place = jnp.where(owned_grid, rank, capacity)
    group_rows = jnp.broadcast_to(jnp.arange(groups, dtype=jnp.int32)[:, None], (groups, tok_rows))
    row_of = (
        jnp.zeros((groups, capacity), jnp.int32)
        .at[group_rows, place]
        .set(line_idx.reshape(groups, tok_rows), mode="drop")
    )
    filled = jnp.zeros((groups, capacity), jnp.bool_).at[group_rows, place].set(True, mode="drop")
    fetched = jnp.take(table, row_of.reshape(-1), axis=0).reshape(groups, capacity, width)
    fetched = jnp.where(filled[:, :, None], fetched, jnp.zeros((), jnp.bfloat16))
    arrived = lax.all_to_all(fetched, "dp", split_axis=0, concat_axis=0, tiled=True)
    my_local = token_ids - first
    my_in = (my_local >= 0) & (my_local < lines * PACK)
    my_slot = my_local % PACK
    slot_hits = (my_slot[:, None] == jnp.arange(PACK, dtype=jnp.int32)[None, :]) & my_in[:, None]
    slot_ranks = jnp.cumsum(slot_hits.astype(jnp.int32), axis=0) - 1
    my_rank = jnp.sum(jnp.where(slot_hits, slot_ranks, 0), axis=1)
    sources = my_slot[:, None] * quarters + jnp.arange(quarters, dtype=jnp.int32)[None, :]
    flat_index = jnp.clip(sources * capacity + my_rank[:, None], 0, groups * capacity - 1)
    gathered = jnp.take(
        arrived.reshape(groups * capacity, width), flat_index.reshape(-1), axis=0
    ).reshape(tok_rows, D)
    segment_part = jnp.where(my_in[:, None], gathered.astype(jnp.float32), 0.0)
    slot_place = jnp.where(my_in, my_slot, PACK)
    token_at = (
        jnp.zeros((PACK, capacity), jnp.int32)
        .at[slot_place, my_rank]
        .set(jnp.arange(tok_rows, dtype=jnp.int32), mode="drop")
    )
    valid = jnp.zeros((PACK, capacity), jnp.bool_).at[slot_place, my_rank].set(True, mode="drop")
    grad_pick = jnp.take(whole_grad, token_at.reshape(-1), axis=0).reshape(
        PACK, capacity, quarters, width
    )
    grad_pick = jnp.where(valid[:, :, None, None], grad_pick, jnp.zeros((), jnp.bfloat16))
    grad_send = grad_pick.transpose(0, 2, 1, 3).reshape(groups, capacity, width)
    returned = lax.all_to_all(grad_send, "dp", split_axis=0, concat_axis=0, tiled=True)
    target = jnp.where(filled, row_of, lines)
    accum = (
        jnp.zeros((lines, width), jnp.float32)
        .at[target.reshape(-1)]
        .add(returned.reshape(-1, width).astype(jnp.float32), mode="drop")
    )
    embedded = lax.psum(segment_part.astype(jnp.bfloat16), "segment")
    return (embedded, accum.astype(jnp.bfloat16))


def solution(mesh):
    placed = (P("dp"), P("segment", "dp"), P("dp", "segment"))
    return jax.shard_map(
        body,
        mesh=mesh,
        in_specs=placed,
        out_specs=(P("dp", None), P("segment", "dp")),
        check_vma=False,
    )
```

profile of v0, /device:TPU:0, one launch (start us, length us, event | category | flops | bytes accessed | tf_op | source)
XLA Modules:
  0.0 159.1 jit_solution(7434590179938538914)
XLA Ops:
  7.2 0.0 copy-start.1
  7.2 0.0 copy-start
  7.2 22.6 %all-gather = s32[8,1,128]{2,1,0:T(1,128)S(1)} all-gather(s32[1,1,128]{2,1,0:T(1,128)} %bitcast.39), channel_id=1, replica_groups=mesh['segment'=4,'dp'=8] {'dp'}, dimensions={0}, use_global_device_ids=true | all-gather | bytes 4608 | tf_op jit(solution)/shard_map/all_gather | solution.py:18
  29.8 0.3 copy.12
  30.1 0.3 copy.13
  30.4 23.6 %compare_select_fusion = s32[8,128,1]{2,0,1:T(8,128)S(1)} fusion(pred[8,128,1]{2,0,1:T(8,128)(4,1)S(1)} %copy.13, s32[8,128,1]{2,0,1:T(8,128)S(1)} %copy.12), kind=kOutput, calls=%fused_computation.12 | output fusion | flops 135168 | bytes 9216 | tf_op jit(solution)/shard_map/jit(cumsum)/reduce_window_sum | solution.py:26
  54.0 0.2 copy.14
  54.2 0.8 multiply_reduce_fusion
  55.0 0.1 copy.19
  55.1 0.7 and_reduce_fusion
  55.8 0.1 copy.18
  56.0 4.3 %scatter_custom_fusion.4 = s32[128]{0:T(128)S(1)} fusion(s32[1024]{0:T(1024)S(1)} %bitcast.40, s32[1024]{0:T(1024)S(1)} %fusion.6, s32[]{:T(128)} %constant.70.clone.1), kind=kCustom, calls=%fused_computation.66 | custom fusion | bytes 516
  60.3 0.1 reshape.189
  60.4 4.3 %scatter_custom_fusion.3 = pred[128]{0:T(512)(128)(4,1)S(1)} fusion(s32[1024]{0:T(1024)S(1)} %bitcast.41, pred[1024]{0:T(1024)(128)(4,1)S(1)} %broadcast.224, pred[]{:T(512)} %constant.71.clone.1), kind=kCustom, calls=%fused_computation.56 | custom fusion | bytes 129
  64.8 0.1 reshape.185
  64.9 6.6 %gather_fusion = bf16[128,3584]{1,0:T(8,128)(2,1)S(1)} fusion(bf16[1188,3584]{1,0:T(8,128)(2,1)} %param.6, s32[1024]{0:T(1024)S(1)} %pad_clamp_fusion.2), kind=kCustom, calls=%fused_computation.2 | custom fusion | bytes 1835520 | tf_op jit(solution)/shard_map/jit(_take)/gather | solution.py:35
  71.4 1.1 select_select_fusion
  72.6 3.6 %all-to-all-start = ((bf16[8,16,3584]{2,1,0:T(8,128)(2,1)}), bf16[8,16,3584]{2,1,0:T(8,128)(2,1)S(1)}, u32[]{:S(2)}, u32[]{:S(2)}) async-start(bf16[8,16,3584]{2,1,0:T(8,128)(2,1)} %select_select_fusion), calls=%async_computation | async-start | bytes 1835008 | tf_op jit(solution)/shard_map/all_to_all | solution.py:37
  76.1 0.0 copy-done.1
  76.2 0.1 fusion.4
  76.3 0.2 reduce_window_sum.23
  76.4 0.2 select_reduce_fusion
  76.7 6.4 %scatter_fusion.1 = s32[8,16]{1,0:T(8,128)S(1)} fusion(s32[8,16]{1,0:T(8,128)S(1)} %broadcast.169, s32[128]{0:T(128)S(1)} %fusion.18, s32[128]{0:T(128)S(1)} %iota.14), kind=kCustom, calls=%fused_computation.4 | custom fusion | bytes 2560 | tf_op jit(solution)/shard_map/scatter | solution.py:54
  83.0 0.1 reshape.180
  83.1 0.0 copy-done
  83.2 9.5 %all_gather.7 = bf16[128,3584]{1,0:T(8,128)(2,1)S(1)} all-gather(bf16[128,896]{1,0:T(8,128)(2,1)S(1)} %copy-done), channel_id=1, replica_groups=mesh['segment'=4,'dp'=8] {'segment'}, dimensions={1}, use_global_device_ids=true | all-gather | bytes 1146880 | tf_op jit(solution)/shard_map/all_gather | solution.py:23
  92.7 1.1 gather_fusion.2
  93.8 6.5 %scatter_fusion = pred[8,16]{1,0:T(8,128)(4,1)S(1)} fusion(pred[8,16]{1,0:T(8,128)(4,1)S(1)} %broadcast.166, s32[128]{0:T(128)S(1)} %fusion.18, pred[128]{0:T(512)(128)(4,1)S(1)} %broadcast.225), kind=kCustom, calls=%fused_computation.3 | custom fusion | bytes 1408 | tf_op jit(solution)/shard_map/scatter | solution.py:56
  100.3 0.2 broadcast_select_fusion
  100.5 1.1 broadcast_select_fusion.1
  101.5 0.0 all-to-all-done
  101.5 5.9 %all-to-all-start.1 = ((bf16[8,16,3584]{2,1,0:T(8,128)(2,1)}), bf16[8,16,3584]{2,1,0:T(8,128)(2,1)S(1)}, u32[]{:S(2)}, u32[]{:S(2)}) async-start(bf16[8,16,3584]{2,1,0:T(8,128)(2,1)} %broadcast_select_fusion.1), calls=%async_computation.1 | async-start | bytes 1835008 | tf_op jit(solution)/shard_map/all_to_all | solution.py:62
  107.5 0.0 all-reduce.2.cloned.1.call-start
  107.5 1.1 gather_fusion.1
  108.7 1.3 select_convert_fusion
  109.9 0.0 all-reduce.2.cloned.1.call-update
  110.0 0.1 reshape.179
  110.1 20.9 %all-to-all-done.1 = bf16[8,16,3584]{2,1,0:T(8,128)(2,1)S(1)} async-done(((bf16[8,16,3584]{2,1,0:T(8,128)(2,1)}), bf16[8,16,3584]{2,1,0:T(8,128)(2,1)S(1)}, u32[]{:S(2)}, u32[]{:S(2)}) %all-to-all-start.1) | async-done | bytes 917536 | tf_op jit(solution)/shard_map/all_to_all | solution.py:62
  130.9 10.0 %scatter_custom_fusion.2 = f32[1188,3584]{1,0:T(8,128)} fusion(s32[128]{0:T(128)S(1)} %fusion.16, f32[]{:T(128)} %constant.121.clone.1, bf16[128,3584]{1,0:T(8,128)(2,1)S(1)} %bitcast.35), kind=kCustom, calls=%fused_computation.8 | custom fusion | flops 917504 | bytes 17948676 | tf_op jit(solution)/shard_map/scatter-add | solution.py:67
  140.9 9.1 %convert_element_type.32 = bf16[1188,3584]{1,0:T(8,128)(2,1)} convert(f32[1188,3584]{1,0:T(8,128)} %scatter_custom_fusion.2) | non-fusion elementwise | flops 4257792 | bytes 25546752 | tf_op jit(solution)/shard_map/convert_element_type | solution.py:70
  150.1 0.0 all-reduce.2.cloned.1.call-done
  150.1 2.2 %copy.23 = bf16[128,3584]{1,0:T(8,128)(2,1)} copy(bf16[128,3584]{1,0:T(8,128)(2,1)} %all-reduce.2.cloned.1.call-done) | data formatting | bytes 1835008
  (24 shorter events, 0.2 us)
Async XLA Ops:
  7.2 69.0 %copy-start.1 = (s32[128]{0:T(128)S(1)}, s32[128]{0:T(128)}, u32[]{:S(2)}) copy-start(s32[128]{0:T(128)} %param.5) | copy-start | bytes 1540
  7.2 76.0 %copy-start = (bf16[128,896]{1,0:T(8,128)(2,1)S(1)}, bf16[128,896]{1,0:T(8,128)(2,1)}, u32[]{:S(2)}) copy-start(bf16[128,896]{1,0:T(8,128)(2,1)} %param.7) | copy-start | bytes 688132
  72.6 29.0 %all-to-all-start = ((bf16[8,16,3584]{2,1,0:T(8,128)(2,1)}), bf16[8,16,3584]{2,1,0:T(8,128)(2,1)S(1)}, u32[]{:S(2)}, u32[]{:S(2)}) async-start(bf16[8,16,3584]{2,1,0:T(8,128)(2,1)} %select_select_fusion), calls=%async_computation | async-start | bytes 1835008 | tf_op jit(solution)/shard_map/all_to_all | solution.py:37
  101.5 29.4 %all-to-all-start.1 = ((bf16[8,16,3584]{2,1,0:T(8,128)(2,1)}), bf16[8,16,3584]{2,1,0:T(8,128)(2,1)S(1)}, u32[]{:S(2)}, u32[]{:S(2)}) async-start(bf16[8,16,3584]{2,1,0:T(8,128)(2,1)} %broadcast_select_fusion.1), calls=%async_computation.1 | async-start | bytes 1835008 | tf_op jit(solution)/shard_map/all_to_all | solution.py:62
  107.5 42.6 %all-reduce.2.cloned.1.call-start = ((), (), s32[]{:S(2)}) async-start(), calls=%async_computation.2 | async-start | bytes 1835008 | tf_op jit(solution)/shard_map/psum | solution.py:69
Sparse Core Ops, SparseCore 0:
  111.2 36.2 all-reduce.1
where the time goes:
time: 159 us
  other arithmetic  48.5 us (31%)
  local copies, waits for them, and re-layouts  33.8 us (21%)
  blocking collectives  32.1 us (20%)
  waiting for transfers between devices  20.9 us (13%)
  between operations  14.3 us (9%)
  starting transfers between devices  9.52 us (6%)
    another operation x1, other arithmetic, body(): rank = jnp.cumsum(owned_grid.astype(jnp.int32), axis=1) - 1  23.6 us
    all_gather x1, blocking collectives, body(): every_id = lax.all_gather(token_ids, 'dp', axis=0, tiled=True)  22.6 us
    all_to_all x1, waiting for transfers between devices, body(): lax.all_to_all(grad_send, 'dp', split_axis=0, concat_axis=0, tiled=True)  20.9 us
    unnamed x11, local copies, waits for them, and re-layouts  11.1 us
    scatter-add x1, other arithmetic, body(): accum = jnp.zeros((lines, width), jnp.float32).at[target.reshape(-1)].add...  10 us
    all_gather x1, blocking collectives, body(): whole_grad = lax.all_gather(out_grad, 'segment', axis=1, tiled=True)  9.52 us
    convert_element_type x1, other arithmetic, body(): return (embedded, accum.astype(jnp.bfloat16))  9.14 us
    gather x1, local copies, waits for them, and re-layouts, body(): jnp.take(table, row_of.reshape(-1), axis=0).reshape(groups, capacity, width)  6.55 us
  transfers between devices with their start and end apart: 3, of which 1 were waited for; matrix products, arithmetic and copies ran while one was open for 24% of the time, Pallas kernels for 0%

commit v1 on v0

--- a/solution.py
+++ b/solution.py
@@ -20,7 +20,7 @@
     in_section = (local >= 0) & (local < lines * PACK)
     owned = in_section & (local % PACK == slot)
     line_idx = jnp.clip(local // PACK, 0, lines - 1)
-    whole_grad = lax.all_gather(out_grad, "segment", axis=1, tiled=True)
+    whole_grad = jnp.concatenate(lax.all_gather(out_grad, "segment"), axis=1)
     capacity = tok_rows // PACK
     owned_grid = owned.reshape(groups, tok_rows)
     rank = jnp.cumsum(owned_grid.astype(jnp.int32), axis=1) - 1

time: 159 us -> 160 us (level)
    unnamed x11 -> x12, local copies, waits for them, and re-layouts: 11.1 us -> 11.2 us
where the time goes in v1:
time: 160 us
  other arithmetic  48.5 us (30%)
  local copies, waits for them, and re-layouts  34.6 us (22%)
  blocking collectives  32.1 us (20%)
  waiting for transfers between devices  20.9 us (13%)
  between operations  14.3 us (9%)
  starting transfers between devices  9.52 us (6%)
    another operation x1, other arithmetic, body(): rank = jnp.cumsum(owned_grid.astype(jnp.int32), axis=1) - 1  23.6 us
    all_gather x1, blocking collectives, body(): every_id = lax.all_gather(token_ids, 'dp', axis=0, tiled=True)  22.6 us
    all_to_all x1, waiting for transfers between devices, body(): lax.all_to_all(grad_send, 'dp', split_axis=0, concat_axis=0, tiled=True)  20.9 us
    unnamed x12, local copies, waits for them, and re-layouts  11.2 us
    scatter-add x1, other arithmetic, body(): accum = jnp.zeros((lines, width), jnp.float32).at[target.reshape(-1)].add...  10 us
    all_gather x1, blocking collectives, body(): whole_grad = jnp.concatenate(lax.all_gather(out_grad, 'segment'), axis=1)  9.52 us
    convert_element_type x1, other arithmetic, body(): return (embedded, accum.astype(jnp.bfloat16))  9.14 us
    gather x1, local copies, waits for them, and re-layouts, body(): jnp.take(table, row_of.reshape(-1), axis=0).reshape(groups, capacity, width)  6.55 us
  transfers between devices with their start and end apart: 3, of which 1 were waited for; matrix products, arithmetic and copies ran while one was open for 24% of the time, Pallas kernels for 0%

profile of v1, /device:TPU:0, one launch (start us, length us, event | category | flops | bytes accessed | tf_op | source)
XLA Modules:
  0.0 159.9 jit_solution(10123239750079881271)
XLA Ops:
  7.2 0.0 copy-start.1
  7.2 0.0 copy-start
  7.2 22.6 %all-gather.1 = s32[8,1,128]{2,1,0:T(1,128)S(1)} all-gather(s32[1,1,128]{2,1,0:T(1,128)} %bitcast.46), channel_id=1, replica_groups=mesh['segment'=4,'dp'=8] {'dp'}, dimensions={0}, use_global_device_ids=true | all-gather | bytes 4608 | tf_op jit(solution)/shard_map/all_gather | solution.py:18
  29.8 0.3 copy.15
  30.1 0.3 copy.16
  30.4 23.6 %compare_select_fusion = s32[8,128,1]{2,0,1:T(8,128)S(1)} fusion(pred[8,128,1]{2,0,1:T(8,128)(4,1)S(1)} %copy.16, s32[8,128,1]{2,0,1:T(8,128)S(1)} %copy.15), kind=kOutput, calls=%fused_computation.12 | output fusion | flops 135168 | bytes 9216 | tf_op jit(solution)/shard_map/jit(cumsum)/reduce_window_sum | solution.py:26
  54.0 0.2 copy.17
  54.2 0.8 multiply_reduce_fusion
  55.0 0.1 copy.23
  55.1 0.7 and_reduce_fusion
  55.8 0.1 copy.22
  56.0 4.3 %scatter_custom_fusion.4 = s32[128]{0:T(128)S(1)} fusion(s32[1024]{0:T(1024)S(1)} %bitcast.47, s32[1024]{0:T(1024)S(1)} %fusion.6, s32[]{:T(128)} %constant.70.clone.1), kind=kCustom, calls=%fused_computation.66 | custom fusion | bytes 516
  60.3 0.1 reshape.197
  60.4 4.3 %scatter_custom_fusion.3 = pred[128]{0:T(512)(128)(4,1)S(1)} fusion(s32[1024]{0:T(1024)S(1)} %bitcast.48, pred[1024]{0:T(1024)(128)(4,1)S(1)} %broadcast.224, pred[]{:T(512)} %constant.71.clone.1), kind=kCustom, calls=%fused_computation.56 | custom fusion | bytes 129
  64.8 0.1 reshape.193
  64.9 6.6 %gather_fusion = bf16[128,3584]{1,0:T(8,128)(2,1)S(1)} fusion(bf16[1188,3584]{1,0:T(8,128)(2,1)} %param.6, s32[1024]{0:T(1024)S(1)} %pad_clamp_fusion.2), kind=kCustom, calls=%fused_computation.2 | custom fusion | bytes 1835520 | tf_op jit(solution)/shard_map/jit(_take)/gather | solution.py:35
  71.4 1.1 select_select_fusion
  72.6 3.6 %all-to-all-start = ((bf16[8,16,3584]{2,1,0:T(8,128)(2,1)}), bf16[8,16,3584]{2,1,0:T(8,128)(2,1)S(1)}, u32[]{:S(2)}, u32[]{:S(2)}) async-start(bf16[8,16,3584]{2,1,0:T(8,128)(2,1)} %select_select_fusion), calls=%async_computation | async-start | bytes 1835008 | tf_op jit(solution)/shard_map/all_to_all | solution.py:37
  76.1 0.0 copy-done.1
  76.2 0.1 fusion.4
  76.3 0.2 reduce_window_sum.23
  76.4 0.2 select_reduce_fusion
  76.7 6.4 %scatter_fusion.1 = s32[8,16]{1,0:T(8,128)S(1)} fusion(s32[8,16]{1,0:T(8,128)S(1)} %broadcast.169, s32[128]{0:T(128)S(1)} %fusion.18, s32[128]{0:T(128)S(1)} %iota.14), kind=kCustom, calls=%fused_computation.4 | custom fusion | bytes 2560 | tf_op jit(solution)/shard_map/scatter | solution.py:54
  83.0 0.1 reshape.188
  83.1 0.0 copy-done
  83.2 9.5 %all-gather = bf16[512,896]{1,0:T(8,128)(2,1)S(1)} all-gather(bf16[128,896]{1,0:T(8,128)(2,1)S(1)} %copy-done), channel_id=2, replica_groups=mesh['segment'=4,'dp'=8] {'segment'}, dimensions={0}, use_global_device_ids=true | all-gather | bytes 1146880 | tf_op jit(solution)/shard_map/all_gather | solution.py:23
  92.7 0.7 copy.21
  93.4 0.1 copy.24
  93.5 1.1 gather_fusion.2
  94.7 6.5 %scatter_fusion = pred[8,16]{1,0:T(8,128)(4,1)S(1)} fusion(pred[8,16]{1,0:T(8,128)(4,1)S(1)} %broadcast.166, s32[128]{0:T(128)S(1)} %fusion.18, pred[128]{0:T(512)(128)(4,1)S(1)} %broadcast.225), kind=kCustom, calls=%fused_computation.3 | custom fusion | bytes 1408 | tf_op jit(solution)/shard_map/scatter | solution.py:56
  101.1 0.2 broadcast_select_fusion
  101.3 1.1 broadcast_select_fusion.1
  102.4 0.0 all-to-all-done
  102.4 5.9 %all-to-all-start.1 = ((bf16[8,16,3584]{2,1,0:T(8,128)(2,1)}), bf16[8,16,3584]{2,1,0:T(8,128)(2,1)S(1)}, u32[]{:S(2)}, u32[]{:S(2)}) async-start(bf16[8,16,3584]{2,1,0:T(8,128)(2,1)} %broadcast_select_fusion.1), calls=%async_computation.1 | async-start | bytes 1835008 | tf_op jit(solution)/shard_map/all_to_all | solution.py:62
  108.3 0.0 all-reduce.2.cloned.1.call-start
  108.4 1.1 gather_fusion.1
  109.5 1.3 select_convert_fusion
  110.8 0.0 all-reduce.2.cloned.1.call-update
  110.8 0.1 reshape.185
  110.9 20.9 %all-to-all-done.1 = bf16[8,16,3584]{2,1,0:T(8,128)(2,1)S(1)} async-done(((bf16[8,16,3584]{2,1,0:T(8,128)(2,1)}), bf16[8,16,3584]{2,1,0:T(8,128)(2,1)S(1)}, u32[]{:S(2)}, u32[]{:S(2)}) %all-to-all-start.1) | async-done | bytes 917536 | tf_op jit(solution)/shard_map/all_to_all | solution.py:62
  131.7 10.0 %scatter_custom_fusion.2 = f32[1188,3584]{1,0:T(8,128)} fusion(s32[128]{0:T(128)S(1)} %fusion.16, f32[]{:T(128)} %constant.121.clone.1, bf16[128,3584]{1,0:T(8,128)(2,1)S(1)} %bitcast.42), kind=kCustom, calls=%fused_computation.8 | custom fusion | flops 917504 | bytes 17948676 | tf_op jit(solution)/shard_map/scatter-add | solution.py:67
  141.8 9.1 %convert_element_type.32 = bf16[1188,3584]{1,0:T(8,128)(2,1)} convert(f32[1188,3584]{1,0:T(8,128)} %scatter_custom_fusion.2) | non-fusion elementwise | flops 4257792 | bytes 25546752 | tf_op jit(solution)/shard_map/convert_element_type | solution.py:70
  150.9 0.0 all-reduce.2.cloned.1.call-done
  150.9 2.2 %copy.28 = bf16[128,3584]{1,0:T(8,128)(2,1)} copy(bf16[128,3584]{1,0:T(8,128)(2,1)} %all-reduce.2.cloned.1.call-done) | data formatting | bytes 1835008
  (24 shorter events, 0.2 us)
Async XLA Ops:
  7.2 69.0 %copy-start.1 = (s32[128]{0:T(128)S(1)}, s32[128]{0:T(128)}, u32[]{:S(2)}) copy-start(s32[128]{0:T(128)} %param.5) | copy-start | bytes 1540
  7.2 76.0 %copy-start = (bf16[128,896]{1,0:T(8,128)(2,1)S(1)}, bf16[128,896]{1,0:T(8,128)(2,1)}, u32[]{:S(2)}) copy-start(bf16[128,896]{1,0:T(8,128)(2,1)} %param.7) | copy-start | bytes 688132
  72.6 29.8 %all-to-all-start = ((bf16[8,16,3584]{2,1,0:T(8,128)(2,1)}), bf16[8,16,3584]{2,1,0:T(8,128)(2,1)S(1)}, u32[]{:S(2)}, u32[]{:S(2)}) async-start(bf16[8,16,3584]{2,1,0:T(8,128)(2,1)} %select_select_fusion), calls=%async_computation | async-start | bytes 1835008 | tf_op jit(solution)/shard_map/all_to_all | solution.py:37
  102.4 29.4 %all-to-all-start.1 = ((bf16[8,16,3584]{2,1,0:T(8,128)(2,1)}), bf16[8,16,3584]{2,1,0:T(8,128)(2,1)S(1)}, u32[]{:S(2)}, u32[]{:S(2)}) async-start(bf16[8,16,3584]{2,1,0:T(8,128)(2,1)} %broadcast_select_fusion.1), calls=%async_computation.1 | async-start | bytes 1835008 | tf_op jit(solution)/shard_map/all_to_all | solution.py:62
  108.3 42.6 %all-reduce.2.cloned.1.call-start = ((), (), s32[]{:S(2)}) async-start(), calls=%async_computation.2 | async-start | bytes 1835008 | tf_op jit(solution)/shard_map/psum | solution.py:69
Sparse Core Ops, SparseCore 0:
  112.0 36.2 all-reduce.1
